TPU v7x, 32 devices: a whole 2x2x4 slice. The times are simulated.
32 devices in a mesh: dp: 8 (over z, y), rep: 4 (over x, core).
Axes of the slice: x: 2, y: 2, z: 4, core: 2. Of those that a mesh axis runs over, the one named last changes fastest.
Arguments:
- grads: bfloat16 [32, 4096, 512], P(('dp', 'rep')), may hold values from -1000 to 1000
- master: float32 [4096, 512], P('dp'), may hold values from -3 to 3
- first_moment: float32 [4096, 512], P('dp'), may hold values from -2 to 2
- second_moment: float32 [4096, 512], P('dp'), may hold values from 0.01 to 1
Outputs:
- weights: bfloat16 [4096, 512], replicated
- new_master: float32 [4096, 512], P('dp')
- new_first: float32 [4096, 512], P('dp')
- new_second: float32 [4096, 512], P('dp')
All inputs are finite; a program needn't handle non-finite values.
Results may differ from a plain program's by a relative error of at most 0.001.
Values may be sent and summed in bfloat16 or wider, within the bound.
A program may use at most 64 MiB of HBM per device.

v0:
```python
import math

import jax
import jax.numpy as jnp
from jax import lax
from jax.sharding import PartitionSpec as P

D_WIN = 4096
STEP = 20


def adam_update(clipped, master, first_moment, second_moment):
    new_first = 0.9 * first_moment + 0.1 * clipped
    new_second = 0.95 * second_moment + 0.05 * clipped * clipped
    first_hat = new_first / (1.0 - 0.9**STEP)
    second_hat = new_second / (1.0 - 0.95**STEP)
    update = first_hat / (jnp.sqrt(second_hat) + 1e-08)
    new_master = master - 0.01 * (update + 0.1 * master)
    return (new_master, new_first, new_second)


def clip_factor(squares, width):
    threshold = 4.0 * math.sqrt(D_WIN * width)
    return jnp.minimum(1.0, threshold / (jnp.sqrt(squares) + 1e-06))


def body(grads, master, first_moment, second_moment):
    width = grads.shape[2]
    local = grads[0].astype(jnp.float32)
    pieces = lax.psum_scatter(local, ("dp", "rep"), scatter_dimension=0, tiled=True)
    squares = lax.psum(jnp.sum(pieces * pieces), ("dp", "rep"))
    summed = lax.all_gather(pieces, "rep", axis=0, tiled=True)
    factor = clip_factor(squares, width)
    new_master, new_first, new_second = adam_update(
        factor * summed, master, first_moment, second_moment
    )
    weights = lax.all_gather(new_master.astype(jnp.bfloat16), "dp", axis=0, tiled=True)
    return (weights, new_master, new_first, new_second)


def solution(mesh):
    in_specs = (P(("dp", "rep"), None, None), P("dp", None), P("dp", None), P("dp", None))
    out_specs = (P(), P("dp", None), P("dp", None), P("dp", None))
    return jax.shard_map(body, mesh=mesh, in_specs=in_specs, out_specs=out_specs, check_vma=False)
```

profile of v0, /device:TPU:1, one launch (start us, length us, event | category | flops | bytes accessed | tf_op | source)
XLA Modules:
  0.0 293.0 jit_solution(11010574628274606125)
XLA Ops:
  7.2 0.0 reduce-scatter.2.cloned.1.call-start
  7.2 6.6 %bitcast_convert_fusion = f32[4096,512]{1,0:T(8,128)} fusion(bf16[1,4096,512]{2,1,0:T(8,128)(2,1)} %param.4), kind=kLoop, calls=%fused_computation | loop fusion | flops 2097152 | bytes 12582912 | tf_op jit(solution)/shard_map/convert_element_type | solution.py:29
  13.8 0.0 copy-start
  13.8 0.0 copy-start.1
  13.8 0.0 copy-start.2
  13.8 0.0 reduce-scatter.2.cloned.1.call-update
  13.8 0.0 all-gather.3.cloned.1.call-start
  13.9 146.9 %reduce-scatter.2.cloned.1.call-done = f32[128,512]{1,0:T(8,128)} async-done(((f32[4096,512]{1,0:T(8,128)}), f32[128,512]{1,0:T(8,128)}) %reduce-scatter.2.cloned.1.call-update) | async-done | bytes 262160 | tf_op jit(solution)/shard_map/reduce_scatter | solution.py:30
  160.8 0.0 all-gather.3.cloned.1.call-update
  160.8 0.0 all-gather.5.cloned.1.call-start
  160.8 1.6 multiply_reduce_fusion
  162.5 42.1 %psum.7 = f32[]{:T(128)} all-reduce(f32[]{:T(128)} %multiply_reduce_fusion), channel_id=1, replica_groups=mesh['dp'=8,'rep'=4] {'dp','rep'}, use_global_device_ids=true, to_apply=%region_2.0 | all-reduce | flops 1 | bytes 8 | tf_op jit(solution)/shard_map/psum | solution.py:31
  205.3 0.0 all-gather.3.cloned.1.call-done
  205.3 0.0 copy-done
  205.3 0.0 copy-done.1
  205.3 0.0 copy-done.2
  205.3 3.6 %fusion.1 = (bf16[512,512]{1,0:T(8,128)(2,1)}, f32[512,512]{1,0:T(8,128)}, f32[512,512]{1,0:T(8,128)}, f32[512,512]{1,0:T(8,128)}) fusion(f32[512,512]{1,0:T(8,128)S(1)} %copy-done, f32[512,512]{1,0:T(8,128)} %all-gather.3.cloned.1.call-done, f32[]{:T(128)S(6)} %min_shard_map.3, f32[512,512]{1,0:T(8,128)S(1)} %copy-done.1, f32[512,512]{1,0:T(8,128)S(1)} %copy-done.2), kind=kLoop, calls=%fused_computation.6 | loop fusion | flops 4456448 | bytes 7864324 | tf_op jit(solution)/shard_map/convert_element_type | solution.py:37
  209.0 0.0 all-gather.5.cloned.1.call-update
  209.0 73.0 %all-gather.5.cloned.1.call-done = bf16[4096,512]{1,0:T(8,128)(2,1)} async-done(((bf16[512,512]{1,0:T(8,128)(2,1)}), bf16[4096,512]{1,0:T(8,128)(2,1)}) %all-gather.5.cloned.1.call-update) | async-done | bytes 4194320 | tf_op jit(solution)/shard_map/all_gather | solution.py:37
  282.0 4.5 %copy.9 = bf16[4096,512]{1,0:T(8,128)(2,1)} copy(bf16[4096,512]{1,0:T(8,128)(2,1)} %all-gather.5.cloned.1.call-done) | data formatting | bytes 8388608
Async XLA Ops:
  7.2 153.6 %reduce-scatter.2.cloned.1.call-start = ((), (), s32[]{:S(2)}) async-start(), calls=%async_computation.1 | async-start | bytes 8650752 | tf_op jit(solution)/shard_map/reduce_scatter | solution.py:30
  13.8 191.5 %copy-start = (f32[512,512]{1,0:T(8,128)S(1)}, f32[512,512]{1,0:T(8,128)}, u32[]{:S(2)}) copy-start(f32[512,512]{1,0:T(8,128)} %param.5) | copy-start | bytes 3145732
  13.8 191.5 %copy-start.1 = (f32[512,512]{1,0:T(8,128)S(1)}, f32[512,512]{1,0:T(8,128)}, u32[]{:S(2)}) copy-start(f32[512,512]{1,0:T(8,128)} %param.6) | copy-start | bytes 3145732
  13.8 191.5 %copy-start.2 = (f32[512,512]{1,0:T(8,128)S(1)}, f32[512,512]{1,0:T(8,128)}, u32[]{:S(2)}) copy-start(f32[512,512]{1,0:T(8,128)} %param.7) | copy-start | bytes 3145732
  13.8 191.4 %all-gather.3.cloned.1.call-start = ((), (), s32[]{:S(2)}) async-start(), calls=%async_computation.2 | async-start | bytes 1310720 | tf_op jit(solution)/shard_map/all_gather | solution.py:32
  160.8 121.2 %all-gather.5.cloned.1.call-start = ((), (), s32[]{:S(2)}) async-start(), calls=%async_computation.3 | async-start | bytes 4718592 | tf_op jit(solution)/shard_map/all_gather | solution.py:37
Sparse Core Ops, SparseCore 0:
  14.0 146.7 reduce-scatter.1
  162.3 18.5 all-gather.2
  209.1 72.8 all-gather.4
where the time goes:
time: 295 us; the launch traced here: 293 us
  waiting for transfers between devices  220 us (75%)
  blocking collectives  42.1 us (14%)
  between operations  14.5 us (5%)
  other arithmetic  11.9 us (4%)
  local copies, waits for them, and re-layouts  4.48 us (2%)
    reduce_scatter x1, waiting for transfers between devices, body(): lax.psum_scatter(local, ('dp', 'rep'), scatter_dimension=0, tiled=True)  147 us
    all_gather x1, waiting for transfers between devices, body(): lax.all_gather(new_master.astype(jnp.bfloat16), 'dp', axis=0, tiled=True)  73 us
    psum x1, blocking collectives, body(): squares = lax.psum(jnp.sum(pieces * pieces), ('dp', 'rep'))  42.1 us
    convert_element_type x1, other arithmetic, body(): local = grads[0].astype(jnp.float32)  6.61 us
  transfers between devices with their start and end apart: 3, of which 2 were waited for; matrix products, arithmetic and copies ran while one was open for 1% of the time, Pallas kernels for 0%

commit v1 on v0

v1 whole, which is shorter than its diff:
```python
import functools
import math

import jax
import jax.numpy as jnp
from jax import lax
from jax.experimental import pallas as pl
from jax.experimental.pallas import tpu as pltpu
from jax.sharding import PartitionSpec as P

STEP = 20
MESH = pl.DeviceIdType.MESH
F32 = jnp.float32


def adam_update(clipped, master, first_moment, second_moment):
    new_first = 0.9 * first_moment + 0.1 * clipped
    new_second = 0.95 * second_moment + 0.05 * clipped * clipped
    first_hat = new_first / (1.0 - 0.9**STEP)
    second_hat = new_second / (1.0 - 0.95**STEP)
    update = first_hat / (jnp.sqrt(second_hat) + 1e-08)
    new_master = master - 0.01 * (update + 0.1 * master)
    return (new_master, new_first, new_second)


def clip_factor(squares, entries):
    threshold = 4.0 * math.sqrt(entries)
    return jnp.minimum(1.0, threshold / (jnp.sqrt(squares) + 1e-06))


def kernel(
    Z, R, entries,
    g, m_in, f_in, s_in,
    w_out, m_out, f_out, s_out,
    mine, swapped, S, RA, RB, R2, R3, V, N, M, F, Q, W,
    load_sem, state_sem, out_sem, wout_sem,
    g_sem, a1_sem, b1_sem, a2_sem, b2_sem, z_sem, n_sem, v_sem,
    gz_sem, ga_sem, gb_sem, ha_sem, hb_sem, gc_sem,
):
    D = 2 * Z
    n = D * R
    d, r = lax.axis_index("dp"), lax.axis_index("rep")
    z, y = d // 2, d % 2
    x, c = r // 2, r % 2
    me = d * R + r
    to_x = (d, (1 - x) * 2 + c)
    to_y = (z * 2 + 1 - y, r)
    to_c = (d, x * 2 + 1 - c)

    def to_z(other):
        return (other * 2 + y, r)

    def push(src, dst, sems, index, device):
        return pltpu.make_async_remote_copy(
            src_ref=src, dst_ref=dst, send_sem=sems.at[(0,) + index], recv_sem=sems.at[(1,) + index],
            device_id=device, device_id_type=MESH,
        )

    def dest(k):
        return (z + 1 + k) % Z

    barrier = pltpu.get_barrier_semaphore()

    @pl.loop(1, n)
    def _(k):
        t = (me + k) % n
        pl.semaphore_signal(barrier, inc=1, device_id=(t // R, t % R), device_id_type=MESH)

    def load(k):
        return pltpu.make_async_copy(g.at[dest(k), :, c], mine.at[k], load_sem.at[k])

    @pl.loop(0, Z)
    def _(k):
        load(k).start()

    states = [
        pltpu.make_async_copy(a, b, state_sem.at[i])
        for i, (a, b) in enumerate([(m_in, M), (f_in, F), (s_in, Q)])
    ]
    for copy in states:
        copy.start()
    pl.semaphore_wait(barrier, n - 1)

    def swap(k):
        return push(g.at[dest(k), :, 1 - c], swapped.at[k], g_sem, (k,), to_c)

    @pl.loop(0, Z)
    def _(k):
        swap(k).start()

    def first_a(k):
        return push(S.at[k, :, 1 - x, 0], RA.at[k], a1_sem, (k,), to_x)

    def first_b(k):
        return push(S.at[k, 1 - y, :, 1], RB.at[k], b1_sem, (k,), to_y)

    def second_a(k):
        return push(S.at[k, 1 - y, x, 0], R2.at[k, 0], a2_sem, (k,), to_y)

    def second_b(k):
        return push(S.at[k, y, 1 - x, 1], R2.at[k, 1], b2_sem, (k,), to_x)

    def along_z(k):
        return push(S.at[k, y, x], R3.at[k], z_sem, (k,), to_z(dest(k)))

    @pl.loop(0, Z + 2)
    def _(step):
        @pl.when(step < Z)
        def _():
            k = step
            load(k).wait()
            swap(k).wait_recv()
            S[k] = mine[k].astype(F32) + swapped[k].astype(F32)
            first_a(k).start()
            first_b(k).start()

        @pl.when((step >= 1) & (step < Z + 1))
        def _():
            k = step - 1
            first_a(k).wait_recv()
            S[k, :, x, 0] = S[k, :, x, 0] + RA[k]
            second_a(k).start()
            first_b(k).wait_recv()
            S[k, y, :, 1] = S[k, y, :, 1] + RB[k]
            second_b(k).start()

        @pl.when(step >= 2)
        def _():
            k = step - 2
            second_a(k).wait_recv()
            second_b(k).wait_recv()
            S[k, y, x] = S[k, y, x] + R2[k]

            @pl.when(k < Z - 1)
            def _():
                along_z(k).start()

    @pl.loop(0, Z - 1)
    def _(k):
        along_z(k).wait_recv()
        S[Z - 1, y, x] = S[Z - 1, y, x] + R3[k]

    total = S[Z - 1, y, x]
    V[c, x] = total
    lanes = jnp.sum((total * total).reshape(-1, total.shape[-1]), axis=0, keepdims=True)
    N[me] = sum(lanes[:, i : i + 128] for i in range(0, total.shape[-1], 128))

    def norm_part(k):
        t = (me + k) % n
        return push(N.at[me], N.at[me], n_sem, (k,), (t // R, t % R))

    def norm_recv(k):
        t = (me + n - k) % n
        return push(N.at[t], N.at[t], n_sem, (k,), (t // R, t % R))

    @pl.loop(1, n)
    def _(k):
        norm_part(k).start()

    v_x = push(V.at[c, x], V.at[c, x], v_sem, (0,), to_x)
    v_c = push(V.at[c, x], V.at[c, x], v_sem, (1,), to_c)
    v_xc = push(V.at[c, 1 - x], V.at[c, 1 - x], v_sem, (2,), to_c)
    got_x = push(V.at[c, 1 - x], V.at[c, 1 - x], v_sem, (0,), to_x)
    got_c = push(V.at[1 - c, x], V.at[1 - c, x], v_sem, (1,), to_c)
    got_xc = push(V.at[1 - c, 1 - x], V.at[1 - c, 1 - x], v_sem, (2,), to_c)
    v_x.start()
    v_c.start()

    for copy in states:
        copy.wait()

    @pl.loop(1, n)
    def _(k):
        norm_recv(k).wait_recv()

    factor = clip_factor(jnp.sum(N[...]), entries)

    def update(cc, xx):
        new_master, new_first, new_second = adam_update(factor * V[cc, xx], M[cc, xx], F[cc, xx], Q[cc, xx])
        M[cc, xx] = new_master
        F[cc, xx] = new_first
        Q[cc, xx] = new_second
        return new_master

    W[z, y, c, x] = update(c, x).astype(jnp.bfloat16)

    def source(b):
        return (z + Z - b) % Z

    def gather_z(j):
        return push(W.at[z, y, c, x], W.at[z, y, c, x], gz_sem, (j,), to_z(dest(j)))

    def got_z(j):
        block = W.at[source(j + 1), y, c, x]
        return push(block, block, gz_sem, (j,), to_z(dest(j)))

    @pl.loop(0, Z - 1)
    def _(j):
        gather_z(j).start()

    def same(ref, sems, b, device):
        return push(ref, ref, sems, (b,), device)

    def ga(b, yy):
        return same(W.at[source(b), yy, c, x, 0], ga_sem, b, to_y)

    def gb(b, xx):
        return same(W.at[source(b), y, c, xx, 1], gb_sem, b, to_x)

    def ha(b, xx):
        return same(W.at[source(b), :, c, xx, 0], ha_sem, b, to_x)

    def hb(b, yy):
        return same(W.at[source(b), yy, c, :, 1], hb_sem, b, to_y)

    def gc(b, cc):
        return same(W.at[source(b), :, cc], gc_sem, b, to_c)

    def w_copy(b):
        return pltpu.make_async_copy(W.at[source(b)], w_out.at[source(b)], wout_sem.at[b])

    @pl.loop(0, Z + 3)
    def _(step):
        @pl.when(step < Z)
        def _():
            b = step

            @pl.when(b >= 1)
            def _():
                got_z(b - 1).wait_recv()

            ga(b, y).start()
            gb(b, x).start()

        @pl.when((step >= 1) & (step < Z + 1))
        def _():
            b = step - 1
            ga(b, 1 - y).wait_recv()
            ha(b, x).start()
            gb(b, 1 - x).wait_recv()
            hb(b, y).start()

        @pl.when(step == 1)
        def _():
            got_x.wait_recv()
            v_xc.start()
            update(c, 1 - x)
            got_c.wait_recv()
            update(1 - c, x)
            got_xc.wait_recv()
            update(1 - c, 1 - x)
            for i, (a, b) in enumerate([(M, m_out), (F, f_out), (Q, s_out)]):
                pltpu.make_async_copy(a, b, out_sem.at[i]).start()

        @pl.when((step >= 2) & (step < Z + 2))
        def _():
            b = step - 2
            ha(b, 1 - x).wait_recv()
            hb(b, 1 - y).wait_recv()
            gc(b, c).start()

        @pl.when(step >= 3)
        def _():
            b = step - 3
            gc(b, 1 - c).wait_recv()
            w_copy(b).start()

    for i, (a, b) in enumerate([(M, m_out), (F, f_out), (Q, s_out)]):
        pltpu.make_async_copy(a, b, out_sem.at[i]).wait()
    v_x.wait_send()
    v_c.wait_send()
    v_xc.wait_send()

    @pl.loop(1, n)
    def _(k):
        norm_part(k).wait_send()

    @pl.loop(0, Z)
    def _(k):
        swap(k).wait_send()
        first_a(k).wait_send()
        first_b(k).wait_send()
        second_a(k).wait_send()
        second_b(k).wait_send()
        ga(k, y).wait_send()
        gb(k, x).wait_send()
        ha(k, x).wait_send()
        hb(k, y).wait_send()
        gc(k, c).wait_send()
        w_copy(k).wait()

    @pl.loop(0, Z - 1)
    def _(k):
        along_z(k).wait_send()
        gather_z(k).wait_send()


def body(D, R, grads, master, first_moment, second_moment):
    rows, cols = grads.shape[1:]
    Z, n = D // 2, D * R
    t = rows // (D * R * 2)
    any_space = pl.BlockSpec(memory_space=pl.ANY)
    bf16 = jnp.bfloat16
    part = (2, 2, 2, t, cols)
    dma = pltpu.SemaphoreType.DMA
    state = jax.ShapeDtypeStruct(part, F32)
    outs = pl.pallas_call(
        functools.partial(kernel, Z, R, rows * cols),
        out_shape=[jax.ShapeDtypeStruct((Z, 2) + part, bf16), state, state, state],
        in_specs=[any_space] * 4,
        out_specs=[any_space] * 4,
        scratch_shapes=[
            pltpu.VMEM((Z,) + part, bf16),
            pltpu.VMEM((Z,) + part, bf16),
            pltpu.VMEM((Z,) + part, F32),
            pltpu.VMEM((Z, 2, t, cols), F32),
            pltpu.VMEM((Z, 2, t, cols), F32),
            pltpu.VMEM((Z, 2, t, cols), F32),
            pltpu.VMEM((Z - 1, 2, t, cols), F32),
            pltpu.VMEM(part, F32),
            pltpu.VMEM((n, 1, 128), F32),
            pltpu.VMEM(part, F32),
            pltpu.VMEM(part, F32),
            pltpu.VMEM(part, F32),
            pltpu.VMEM((Z, 2) + part, bf16),
            dma((Z,)), dma((3,)), dma((3,)), dma((Z,)),
            dma((2, Z)), dma((2, Z)), dma((2, Z)), dma((2, Z)), dma((2, Z)), dma((2, Z)),
            dma((2, n)), dma((2, 3)),
            dma((2, Z)), dma((2, Z)), dma((2, Z)), dma((2, Z)), dma((2, Z)), dma((2, Z)),
        ],
        compiler_params=pltpu.CompilerParams(
            collective_id=0, has_side_effects=True, vmem_limit_bytes=48 * 1024 * 1024
        ),
    )(
        grads.reshape((Z, 2) + part),
        master.reshape(part), first_moment.reshape(part), second_moment.reshape(part),
    )
    weights, new_master, new_first, new_second = outs
    block = (rows // D, cols)
    return (weights.reshape(rows, cols), new_master.reshape(block), new_first.reshape(block), new_second.reshape(block))


def solution(mesh):
    D, R = mesh.shape["dp"], mesh.shape["rep"]
    assert R == 4 and D % 2 == 0
    in_specs = (P(("dp", "rep"), None, None), P("dp", None), P("dp", None), P("dp", None))
    out_specs = (P(), P("dp", None), P("dp", None), P("dp", None))
    return jax.shard_map(
        functools.partial(body, D, R), mesh=mesh, in_specs=in_specs, out_specs=out_specs, check_vma=False
    )
```

time: 295 us -> 95.1 us (0.32)
  waiting for transfers between devices: 220 us -> 0 us
  Pallas kernels: 0 us -> 84.1 us
  blocking collectives: 42.1 us -> 0 us
  between operations: 14.5 us -> 0.65 us
  other arithmetic: 11.9 us -> 0 us
  local copies, waits for them, and re-layouts: 4.48 us -> 9.82 us
    reduce_scatter x1 -> x0, waiting for transfers between devices: 147 us -> none  [body(): lax.psum_scatter(local, ('dp', 'rep'), scatter_dimension=0, tiled=True)]
    pallas_call x0 -> x1, Pallas kernels: none -> 84.1 us  [body(): pl.pallas_call(functools.partial(kernel, Z, R, rows * cols), out_shape=[j...]
    all_gather x2 -> x0, waiting for transfers between devices: 73 us -> none  [the longest x1 73 us: body(): lax.all_gather(new_master.astype(jnp.bfloat16), 'dp', axis=0, tiled=True)]
    psum x1 -> x0, blocking collectives: 42.1 us -> none  [body(): squares = lax.psum(jnp.sum(pieces * pieces), ('dp', 'rep'))]
    convert_element_type x2 -> x0, other arithmetic: 10.2 us -> none  [the longest x1 6.61 us: body(): local = grads[0].astype(jnp.float32)]
    unnamed x7 -> x8, local copies, waits for them, and re-layouts: 4.48 us -> 9.82 us
  transfers between devices with their start and end apart: 3 -> 0, of which waited for: 2 -> 0; matrix products, arithmetic and copies ran while one was open for 1% -> 0% of each run, Pallas kernels for 0% -> 0%
where the time goes in v1:
time: 95.1 us; the launch traced here: 94.6 us
  Pallas kernels  84.1 us (88%)
  local copies, waits for them, and re-layouts  9.82 us (10%)
    pallas_call x1, Pallas kernels, body(): pl.pallas_call(functools.partial(kernel, Z, R, rows * cols), out_shape=[j...  84.1 us
    unnamed x8, local copies, waits for them, and re-layouts  9.82 us

profile of v1, /device:TPU:1, one launch (start us, length us, event | category | flops | bytes accessed | tf_op | source)
XLA Modules:
  0.0 94.6 jit_solution(7677623231633569856)
XLA Ops:
  0.6 0.0 copy-start
  0.6 1.2 %copy-done = f32[512,512]{1,0:T(8,128)S(1)} copy-done((f32[512,512]{1,0:T(8,128)S(1)}, f32[512,512]{1,0:T(8,128)}, u32[]{:S(2)}) %copy-start) | copy-done | bytes 1048600
  1.9 0.0 copy-start.1
  1.9 1.2 %copy-done.1 = f32[512,512]{1,0:T(8,128)S(1)} copy-done((f32[512,512]{1,0:T(8,128)S(1)}, f32[512,512]{1,0:T(8,128)}, u32[]{:S(2)}) %copy-start.1) | copy-done | bytes 1048600
  3.1 84.1 %shard_map.75 = (bf16[4,2,2,2,2,64,512]{6,5,4,3,2,1,0:T(8,128)(2,1)}, f32[2,2,2,64,512]{4,3,2,1,0:T(8,128)S(1)}, f32[2,2,2,64,512]{4,3,2,1,0:T(8,128)S(1)}, f32[2,2,2,64,512]{4,3,2,1,0:T(8,128)S(1)}) custom-call(bf16[4,2,2,2,2,64,512]{6,5,4,3,2,1,0:T(8,128)(2,1)} %bitcast.13, f32[2,2,2,64,512]{4,3,2,1,0:T(8,128)S(1)} %bitcast.8, ...), custom_call_target="tpu_custom_call" | custom-call | tf_op jit(solution)/shard_map/pallas_call | solution.py:307
  87.2 4.5 %copy.12 = bf16[4096,512]{1,0:T(8,128)(2,1)} copy(bf16[4096,512]{1,0:T(8,128)(2,1)} %bitcast.14) | data formatting | bytes 8388608
  91.7 1.0 %copy.13 = f32[512,512]{1,0:T(8,128)} copy(f32[512,512]{1,0:T(8,128)S(1)} %bitcast.12) | data formatting | bytes 2097152
  92.7 1.0 %copy.14 = f32[512,512]{1,0:T(8,128)} copy(f32[512,512]{1,0:T(8,128)S(1)} %bitcast.11) | data formatting | bytes 2097152
  93.6 1.0 %copy.15 = f32[512,512]{1,0:T(8,128)} copy(f32[512,512]{1,0:T(8,128)S(1)} %bitcast.10) | data formatting | bytes 2097152
Async XLA Ops:
  0.6 1.2 %copy-start = (f32[512,512]{1,0:T(8,128)S(1)}, f32[512,512]{1,0:T(8,128)}, u32[]{:S(2)}) copy-start(f32[512,512]{1,0:T(8,128)} %param.5) | copy-start | bytes 3145732
  1.9 1.2 %copy-start.1 = (f32[512,512]{1,0:T(8,128)S(1)}, f32[512,512]{1,0:T(8,128)}, u32[]{:S(2)}) copy-start(f32[512,512]{1,0:T(8,128)} %param.6) | copy-start | bytes 3145732

commit v2 on v1

--- a/solution.py
+++ b/solution.py
@@ -11,6 +11,7 @@
 STEP = 20
 MESH = pl.DeviceIdType.MESH
 F32 = jnp.float32
+VMEM_BYTES = 63 * 1024 * 1024
 
 
 def adam_update(clipped, master, first_moment, second_moment):
@@ -31,9 +32,9 @@
 def kernel(
     Z, R, entries,
     g, m_in, f_in, s_in,
-    w_out, m_out, f_out, s_out,
-    mine, swapped, S, RA, RB, R2, R3, V, N, M, F, Q, W,
-    load_sem, state_sem, out_sem, wout_sem,
+    W, M, F, Q,
+    mine, swapped, S, RA, RB, R2, R3, V, N,
+    load_sem, state_sem,
     g_sem, a1_sem, b1_sem, a2_sem, b2_sem, z_sem, n_sem, v_sem,
     gz_sem, ga_sem, gb_sem, ha_sem, hb_sem, gc_sem,
 ):
@@ -216,22 +217,8 @@
     def gc(b, cc):
         return same(W.at[source(b), :, cc], gc_sem, b, to_c)
 
-    def w_copy(b):
-        return pltpu.make_async_copy(W.at[source(b)], w_out.at[source(b)], wout_sem.at[b])
-
-    @pl.loop(0, Z + 3)
+    @pl.loop(0, Z + 2)
     def _(step):
-        @pl.when(step < Z)
-        def _():
-            b = step
-
-            @pl.when(b >= 1)
-            def _():
-                got_z(b - 1).wait_recv()
-
-            ga(b, y).start()
-            gb(b, x).start()
-
         @pl.when((step >= 1) & (step < Z + 1))
         def _():
             b = step - 1
@@ -239,6 +226,17 @@
             ha(b, x).start()
             gb(b, 1 - x).wait_recv()
             hb(b, y).start()
+
+        @pl.when(step < Z)
+        def _():
+            b = step
+
+            @pl.when(b >= 1)
+            def _():
+                got_z(b - 1).wait_recv()
+
+            ga(b, y).start()
+            gb(b, x).start()
 
         @pl.when(step == 1)
         def _():
@@ -249,24 +247,18 @@
             update(1 - c, x)
             got_xc.wait_recv()
             update(1 - c, 1 - x)
-            for i, (a, b) in enumerate([(M, m_out), (F, f_out), (Q, s_out)]):
-                pltpu.make_async_copy(a, b, out_sem.at[i]).start()
-
-        @pl.when((step >= 2) & (step < Z + 2))
+
+        @pl.when(step >= 2)
         def _():
             b = step - 2
             ha(b, 1 - x).wait_recv()
             hb(b, 1 - y).wait_recv()
             gc(b, c).start()
 
-        @pl.when(step >= 3)
-        def _():
-            b = step - 3
-            gc(b, 1 - c).wait_recv()
-            w_copy(b).start()
-
-    for i, (a, b) in enumerate([(M, m_out), (F, f_out), (Q, s_out)]):
-        pltpu.make_async_copy(a, b, out_sem.at[i]).wait()
+    @pl.loop(0, Z)
+    def _(b):
+        gc(b, 1 - c).wait_recv()
+
     v_x.wait_send()
     v_c.wait_send()
     v_xc.wait_send()
@@ -287,28 +279,38 @@
         ha(k, x).wait_send()
         hb(k, y).wait_send()
         gc(k, c).wait_send()
-        w_copy(k).wait()
 
     @pl.loop(0, Z - 1)
     def _(k):
         along_z(k).wait_send()
         gather_z(k).wait_send()
+
+
+def write_out(*refs):
+    srcs, dsts, sems = refs[:4], refs[4:8], refs[8]
+    copies = [pltpu.make_async_copy(a, b, sems.at[i]) for i, (a, b) in enumerate(zip(srcs, dsts))]
+    for copy in copies:
+        copy.start()
+    for copy in copies:
+        copy.wait()
 
 
 def body(D, R, grads, master, first_moment, second_moment):
     rows, cols = grads.shape[1:]
     Z, n = D // 2, D * R
     t = rows // (D * R * 2)
-    any_space = pl.BlockSpec(memory_space=pl.ANY)
+    hbm = pl.BlockSpec(memory_space=pltpu.HBM)
+    vmem = pl.BlockSpec(memory_space=pltpu.VMEM)
     bf16 = jnp.bfloat16
     part = (2, 2, 2, t, cols)
     dma = pltpu.SemaphoreType.DMA
-    state = jax.ShapeDtypeStruct(part, F32)
-    outs = pl.pallas_call(
+    shapes = [((Z, 2) + part, bf16)] + [(part, F32)] * 3
+    held_bytes = sum(math.prod(dims) * jnp.dtype(kind).itemsize for dims, kind in shapes)
+    held = pl.pallas_call(
         functools.partial(kernel, Z, R, rows * cols),
-        out_shape=[jax.ShapeDtypeStruct((Z, 2) + part, bf16), state, state, state],
-        in_specs=[any_space] * 4,
-        out_specs=[any_space] * 4,
+        out_shape=[pltpu.VMEM(*shape) for shape in shapes],
+        in_specs=[hbm] * 4,
+        out_specs=[vmem] * 4,
         scratch_shapes=[
             pltpu.VMEM((Z,) + part, bf16),
             pltpu.VMEM((Z,) + part, bf16),
@@ -319,22 +321,26 @@
             pltpu.VMEM((Z - 1, 2, t, cols), F32),
             pltpu.VMEM(part, F32),
             pltpu.VMEM((n, 1, 128), F32),
-            pltpu.VMEM(part, F32),
-            pltpu.VMEM(part, F32),
-            pltpu.VMEM(part, F32),
-            pltpu.VMEM((Z, 2) + part, bf16),
-            dma((Z,)), dma((3,)), dma((3,)), dma((Z,)),
+            dma((Z,)), dma((3,)),
             dma((2, Z)), dma((2, Z)), dma((2, Z)), dma((2, Z)), dma((2, Z)), dma((2, Z)),
             dma((2, n)), dma((2, 3)),
             dma((2, Z)), dma((2, Z)), dma((2, Z)), dma((2, Z)), dma((2, Z)), dma((2, Z)),
         ],
         compiler_params=pltpu.CompilerParams(
-            collective_id=0, has_side_effects=True, vmem_limit_bytes=48 * 1024 * 1024
+            collective_id=0, has_side_effects=True, vmem_limit_bytes=VMEM_BYTES - held_bytes
         ),
     )(
         grads.reshape((Z, 2) + part),
         master.reshape(part), first_moment.reshape(part), second_moment.reshape(part),
     )
+    outs = pl.pallas_call(
+        write_out,
+        out_shape=[jax.ShapeDtypeStruct(*shape) for shape in shapes],
+        in_specs=[vmem] * 4,
+        out_specs=[hbm] * 4,
+        scratch_shapes=[dma((4,))],
+        compiler_params=pltpu.CompilerParams(vmem_limit_bytes=1024 * 1024),
+    )(*held)
     weights, new_master, new_first, new_second = outs
     block = (rows // D, cols)
     return (weights.reshape(rows, cols), new_master.reshape(block), new_first.reshape(block), new_second.reshape(block))

time: 95.1 us -> 89.5 us (0.941)
  local copies, waits for them, and re-layouts: 9.82 us -> 0 us
  Pallas kernels: 84.1 us -> 88.7 us
    unnamed x8 -> x0, local copies, waits for them, and re-layouts: 9.82 us -> none
    pallas_call x1 -> x2, Pallas kernels: 84.1 us -> 88.7 us  [the longest x1 85.7 us: body(): pl.pallas_call(functools.partial(kernel, Z, R, rows * cols), out_shape=[p...]
where the time goes in v2:
time: 89.5 us; the launch traced here: 89.4 us
  Pallas kernels  88.7 us (99%)
    pallas_call x1, Pallas kernels, body(): pl.pallas_call(functools.partial(kernel, Z, R, rows * cols), out_shape=[p...  85.7 us
    pallas_call x1, Pallas kernels, body(): pl.pallas_call(write_out, out_shape=[jax.ShapeDtypeStruct(*shape) for sha...  3.02 us

profile of v2, /device:TPU:1, one launch (start us, length us, event | category | flops | bytes accessed | tf_op | source)
XLA Modules:
  0.0 89.4 jit_solution(15491320122097285975)
XLA Ops:
  0.6 85.7 %shard_map.75 = (bf16[4,2,2,2,2,64,512]{6,5,4,3,2,1,0:T(8,128)(2,1)S(1)}, f32[2,2,2,64,512]{4,3,2,1,0:T(8,128)S(1)}, f32[2,2,2,64,512]{4,3,2,1,0:T(8,128)S(1)}, f32[2,2,2,64,512]{4,3,2,1,0:T(8,128)S(1)}) custom-call(bf16[4,2,2,2,2,64,512]{6,5,4,3,2,1,0:T(8,128)(2,1)} %bitcast.8, f32[2,2,2,64,512]{4,3,2,1,0:T(8,128)} %bitcast.9, ...), custom_call_target="tpu_custom_call" | custom-call | tf_op jit(solution)/shard_map/pallas_call | solution.py:309
  86.3 3.0 %shard_map.76 = (bf16[4,2,2,2,2,64,512]{6,5,4,3,2,1,0:T(8,128)(2,1)}, f32[2,2,2,64,512]{4,3,2,1,0:T(8,128)}, f32[2,2,2,64,512]{4,3,2,1,0:T(8,128)}, f32[2,2,2,64,512]{4,3,2,1,0:T(8,128)}) custom-call(bf16[4,2,2,2,2,64,512]{6,5,4,3,2,1,0:T(8,128)(2,1)S(1)} %get-tuple-element.12.refs_0_, f32[2,2,2,64,512]{4,3,2,1,0:T(8,128)S(1)} %get-tuple-element.13.refs_1_, ...), custom_call_target="tpu_custom_call" | custom-call | tf_op jit(solution)/shard_map/pallas_call | solution.py:336

commit v3 on v2

--- a/solution.py
+++ b/solution.py
@@ -44,6 +44,8 @@
     z, y = d // 2, d % 2
     x, c = r // 2, r % 2
     me = d * R + r
+    half = g.shape[-1] // 2
+    C = 2 * Z
     to_x = (d, (1 - x) * 2 + c)
     to_y = (z * 2 + 1 - y, r)
     to_c = (d, x * 2 + 1 - c)
@@ -60,6 +62,9 @@
     def dest(k):
         return (z + 1 + k) % Z
 
+    def cols(q):
+        return pl.ds(pl.multiple_of((q % 2) * half, half), half)
+
     barrier = pltpu.get_barrier_semaphore()
 
     @pl.loop(1, n)
@@ -68,9 +73,11 @@
         pl.semaphore_signal(barrier, inc=1, device_id=(t // R, t % R), device_id_type=MESH)
 
     def load(k):
-        return pltpu.make_async_copy(g.at[dest(k), :, c], mine.at[k], load_sem.at[k])
-
-    @pl.loop(0, Z)
+        return pltpu.make_async_copy(
+            g.at[dest(k // 2), :, c, :, :, :, cols(k)], mine.at[k // 2, :, :, :, :, cols(k)], load_sem.at[k]
+        )
+
+    @pl.loop(0, C)
     def _(k):
         load(k).start()
 
@@ -83,63 +90,75 @@
     pl.semaphore_wait(barrier, n - 1)
 
     def swap(k):
-        return push(g.at[dest(k), :, 1 - c], swapped.at[k], g_sem, (k,), to_c)
-
-    @pl.loop(0, Z)
+        return push(
+            g.at[dest(k // 2), :, 1 - c, :, :, :, cols(k)], swapped.at[k // 2, :, :, :, :, cols(k)],
+            g_sem, (k,), to_c,
+        )
+
+    @pl.loop(0, C)
     def _(k):
         swap(k).start()
 
     def first_a(k):
-        return push(S.at[k, :, 1 - x, 0], RA.at[k], a1_sem, (k,), to_x)
+        i, p = k // 2, cols(k)
+        return push(S.at[i, :, 1 - x, 0, :, p], RA.at[i, :, :, p], a1_sem, (k,), to_x)
 
     def first_b(k):
-        return push(S.at[k, 1 - y, :, 1], RB.at[k], b1_sem, (k,), to_y)
+        i, p = k // 2, cols(k)
+        return push(S.at[i, 1 - y, :, 1, :, p], RB.at[i, :, :, p], b1_sem, (k,), to_y)
 
     def second_a(k):
-        return push(S.at[k, 1 - y, x, 0], R2.at[k, 0], a2_sem, (k,), to_y)
+        i, p = k // 2, cols(k)
+        return push(S.at[i, 1 - y, x, 0, :, p], R2.at[i, 0, :, p], a2_sem, (k,), to_y)
 
     def second_b(k):
-        return push(S.at[k, y, 1 - x, 1], R2.at[k, 1], b2_sem, (k,), to_x)
+        i, p = k // 2, cols(k)
+        return push(S.at[i, y, 1 - x, 1, :, p], R2.at[i, 1, :, p], b2_sem, (k,), to_x)
 
     def along_z(k):
-        return push(S.at[k, y, x], R3.at[k], z_sem, (k,), to_z(dest(k)))
-
-    @pl.loop(0, Z + 2)
+        i, p = k // 2, cols(k)
+        return push(S.at[i, y, x, :, :, p], R3.at[i, :, :, p], z_sem, (k,), to_z(dest(i)))
+
+    @pl.loop(0, C + 2)
     def _(step):
-        @pl.when(step < Z)
+        @pl.when(step < C)
         def _():
             k = step
+            i, p = k // 2, cols(k)
             load(k).wait()
             swap(k).wait_recv()
-            S[k] = mine[k].astype(F32) + swapped[k].astype(F32)
+            S[i, :, :, :, :, p] = mine[i, :, :, :, :, p].astype(F32) + swapped[i, :, :, :, :, p].astype(F32)
             first_a(k).start()
             first_b(k).start()
 
-        @pl.when((step >= 1) & (step < Z + 1))
+        @pl.when((step >= 1) & (step < C + 1))
         def _():
             k = step - 1
+            i, p = k // 2, cols(k)
             first_a(k).wait_recv()
-            S[k, :, x, 0] = S[k, :, x, 0] + RA[k]
+            S[i, :, x, 0, :, p] = S[i, :, x, 0, :, p] + RA[i, :, :, p]
             second_a(k).start()
             first_b(k).wait_recv()
-            S[k, y, :, 1] = S[k, y, :, 1] + RB[k]
+            S[i, y, :, 1, :, p] = S[i, y, :, 1, :, p] + RB[i, :, :, p]
             second_b(k).start()
 
         @pl.when(step >= 2)
         def _():
             k = step - 2
+            i, p = k // 2, cols(k)
             second_a(k).wait_recv()
             second_b(k).wait_recv()
-            S[k, y, x] = S[k, y, x] + R2[k]
-
-            @pl.when(k < Z - 1)
+            S[i, y, x, :, :, p] = S[i, y, x, :, :, p] + R2[i, :, :, p]
+
+            @pl.when(k < C - 2)
             def _():
                 along_z(k).start()
 
-    @pl.loop(0, Z - 1)
-    def _(k):
+    @pl.loop(0, C - 2)
+    def _(k):
+        i, p = k // 2, cols(k)
         along_z(k).wait_recv()
-        S[Z - 1, y, x] = S[Z - 1, y, x] + R3[k]
+        S[Z - 1, y, x, :, :, p] = S[Z - 1, y, x, :, :, p] + R3[i, :, :, p]
 
     total = S[Z - 1, y, x]
     V[c, x] = total
@@ -186,16 +205,17 @@
     W[z, y, c, x] = update(c, x).astype(jnp.bfloat16)
 
     def source(b):
-        return (z + Z - b) % Z
+        return (z + Z - b // 2) % Z
 
     def gather_z(j):
-        return push(W.at[z, y, c, x], W.at[z, y, c, x], gz_sem, (j,), to_z(dest(j)))
+        block = W.at[z, y, c, x, :, :, cols(j)]
+        return push(block, block, gz_sem, (j,), to_z(dest(j // 2)))
 
     def got_z(j):
-        block = W.at[source(j + 1), y, c, x]
-        return push(block, block, gz_sem, (j,), to_z(dest(j)))
-
-    @pl.loop(0, Z - 1)
+        block = W.at[source(j + 2), y, c, x, :, :, cols(j)]
+        return push(block, block, gz_sem, (j,), to_z(dest(j // 2)))
+
+    @pl.loop(0, C - 2)
     def _(j):
         gather_z(j).start()
 
@@ -203,23 +223,23 @@
         return push(ref, ref, sems, (b,), device)
 
     def ga(b, yy):
-        return same(W.at[source(b), yy, c, x, 0], ga_sem, b, to_y)
+        return same(W.at[source(b), yy, c, x, 0, :, cols(b)], ga_sem, b, to_y)
 
     def gb(b, xx):
-        return same(W.at[source(b), y, c, xx, 1], gb_sem, b, to_x)
+        return same(W.at[source(b), y, c, xx, 1, :, cols(b)], gb_sem, b, to_x)
 
     def ha(b, xx):
-        return same(W.at[source(b), :, c, xx, 0], ha_sem, b, to_x)
+        return same(W.at[source(b), :, c, xx, 0, :, cols(b)], ha_sem, b, to_x)
 
     def hb(b, yy):
-        return same(W.at[source(b), yy, c, :, 1], hb_sem, b, to_y)
+        return same(W.at[source(b), yy, c, :, 1, :, cols(b)], hb_sem, b, to_y)
 
     def gc(b, cc):
-        return same(W.at[source(b), :, cc], gc_sem, b, to_c)
-
-    @pl.loop(0, Z + 2)
+        return same(W.at[source(b), :, cc, :, :, :, cols(b)], gc_sem, b, to_c)
+
+    @pl.loop(0, C + 2)
     def _(step):
-        @pl.when((step >= 1) & (step < Z + 1))
+        @pl.when((step >= 1) & (step < C + 1))
         def _():
             b = step - 1
             ga(b, 1 - y).wait_recv()
@@ -227,13 +247,13 @@
             gb(b, 1 - x).wait_recv()
             hb(b, y).start()
 
-        @pl.when(step < Z)
+        @pl.when(step < C)
         def _():
             b = step
 
-            @pl.when(b >= 1)
+            @pl.when(b >= 2)
             def _():
-                got_z(b - 1).wait_recv()
+                got_z(b - 2).wait_recv()
 
             ga(b, y).start()
             gb(b, x).start()
@@ -243,8 +263,14 @@
             got_x.wait_recv()
             v_xc.start()
             update(c, 1 - x)
+
+        @pl.when(step == 2)
+        def _():
             got_c.wait_recv()
             update(1 - c, x)
+
+        @pl.when(step == 3)
+        def _():
             got_xc.wait_recv()
             update(1 - c, 1 - x)
 
@@ -255,7 +281,7 @@
             hb(b, 1 - y).wait_recv()
             gc(b, c).start()
 
-    @pl.loop(0, Z)
+    @pl.loop(0, C)
     def _(b):
         gc(b, 1 - c).wait_recv()
 
@@ -267,7 +293,7 @@
     def _(k):
         norm_part(k).wait_send()
 
-    @pl.loop(0, Z)
+    @pl.loop(0, C)
     def _(k):
         swap(k).wait_send()
         first_a(k).wait_send()
@@ -280,7 +306,7 @@
         hb(k, y).wait_send()
         gc(k, c).wait_send()
 
-    @pl.loop(0, Z - 1)
+    @pl.loop(0, C - 2)
     def _(k):
         along_z(k).wait_send()
         gather_z(k).wait_send()
@@ -321,10 +347,10 @@
             pltpu.VMEM((Z - 1, 2, t, cols), F32),
             pltpu.VMEM(part, F32),
             pltpu.VMEM((n, 1, 128), F32),
-            dma((Z,)), dma((3,)),
-            dma((2, Z)), dma((2, Z)), dma((2, Z)), dma((2, Z)), dma((2, Z)), dma((2, Z)),
+            dma((2 * Z,)), dma((3,)),
+            dma((2, 2 * Z)), dma((2, 2 * Z)), dma((2, 2 * Z)), dma((2, 2 * Z)), dma((2, 2 * Z)), dma((2, 2 * Z)),
             dma((2, n)), dma((2, 3)),
-            dma((2, Z)), dma((2, Z)), dma((2, Z)), dma((2, Z)), dma((2, Z)), dma((2, Z)),
+            dma((2, 2 * Z)), dma((2, 2 * Z)), dma((2, 2 * Z)), dma((2, 2 * Z)), dma((2, 2 * Z)), dma((2, 2 * Z)),
         ],
         compiler_params=pltpu.CompilerParams(
             collective_id=0, has_side_effects=True, vmem_limit_bytes=VMEM_BYTES - held_bytes

time: 89.5 us -> 92.2 us (1.030)
  Pallas kernels: 88.7 us -> 91.4 us
    pallas_call x1, Pallas kernels: 85.7 us -> 88.4 us  [body(): pl.pallas_call(functools.partial(kernel, Z, R, rows * cols), out_shape=[p...]
where the time goes in v3:
time: 92.2 us; the launch traced here: 92.1 us
  Pallas kernels  91.4 us (99%)
    pallas_call x1, Pallas kernels, body(): pl.pallas_call(functools.partial(kernel, Z, R, rows * cols), out_shape=[p...  88.4 us
    pallas_call x1, Pallas kernels, body(): pl.pallas_call(write_out, out_shape=[jax.ShapeDtypeStruct(*shape) for sha...  3.02 us

profile of v3, /device:TPU:1, one launch (start us, length us, event | category | flops | bytes accessed | tf_op | source)
XLA Modules:
  0.0 92.1 jit_solution(10566401730764520759)
XLA Ops:
  0.6 88.4 %shard_map.75 = (bf16[4,2,2,2,2,64,512]{6,5,4,3,2,1,0:T(8,128)(2,1)S(1)}, f32[2,2,2,64,512]{4,3,2,1,0:T(8,128)S(1)}, f32[2,2,2,64,512]{4,3,2,1,0:T(8,128)S(1)}, f32[2,2,2,64,512]{4,3,2,1,0:T(8,128)S(1)}) custom-call(bf16[4,2,2,2,2,64,512]{6,5,4,3,2,1,0:T(8,128)(2,1)} %bitcast.8, f32[2,2,2,64,512]{4,3,2,1,0:T(8,128)} %bitcast.9, ...), custom_call_target="tpu_custom_call" | custom-call | tf_op jit(solution)/shard_map/pallas_call | solution.py:335
  89.1 3.0 %shard_map.76 = (bf16[4,2,2,2,2,64,512]{6,5,4,3,2,1,0:T(8,128)(2,1)}, f32[2,2,2,64,512]{4,3,2,1,0:T(8,128)}, f32[2,2,2,64,512]{4,3,2,1,0:T(8,128)}, f32[2,2,2,64,512]{4,3,2,1,0:T(8,128)}) custom-call(bf16[4,2,2,2,2,64,512]{6,5,4,3,2,1,0:T(8,128)(2,1)S(1)} %get-tuple-element.12.refs_0_, f32[2,2,2,64,512]{4,3,2,1,0:T(8,128)S(1)} %get-tuple-element.13.refs_1_, ...), custom_call_target="tpu_custom_call" | custom-call | tf_op jit(solution)/shard_map/pallas_call | solution.py:362
